TPU v7x, 1024 devices: a whole 4x8x16 slice. The times are simulated.
1024 devices in a mesh: gx: 256 (over y, z, core), gy: 4 (over x).
Axes of the slice: x: 4, y: 8, z: 16, core: 2. Of those that a mesh axis runs over, the one named last changes fastest.
Arguments:
- populations: float32 [19, 1024, 32, 128], P(None, 'gx', 'gy'), may hold values from 0.02 to 0.1
- fluid: int32 [1024, 32, 128], P('gx', 'gy'), may hold values 0 or 1
Outputs:
- advanced: float32 [19, 1024, 32, 128], P(None, 'gx', 'gy')
Inputs may be any that keep to these rules, and one draw needn't show every extreme that they name: 1 marks a fluid cell, 0 a solid one.
All inputs are finite; a program needn't handle non-finite values. No bound on the sum of `fluid` on one device may be relied on, other than what follows from the above.
Results may differ from a plain program's by a relative error of at most 0.0001.
Values sent between devices are 32-bit elements; how exact they have to be, the bound alone decides.
A program may use at most 32 MiB of HBM per device.

v0:
```python
import jax
import jax.numpy as jnp
import numpy as np
from jax import lax
from jax.sharding import PartitionSpec as P

STEPS = 4


VELOCITIES = np.array(
    [
        [0, 0, 0],
        [1, 0, 0],
        [-1, 0, 0],
        [0, 1, 0],
        [0, -1, 0],
        [0, 0, 1],
        [0, 0, -1],
        [1, 1, 0],
        [-1, -1, 0],
        [1, -1, 0],
        [-1, 1, 0],
        [1, 0, 1],
        [-1, 0, -1],
        [1, 0, -1],
        [-1, 0, 1],
        [0, 1, 1],
        [0, -1, -1],
        [0, 1, -1],
        [0, -1, 1],
    ]
)
OPPOSITE = [0, 2, 1, 4, 3, 6, 5, 8, 7, 10, 9, 12, 11, 14, 13, 16, 15, 18, 17]
WEIGHTS = [1.0 / 3.0] + [1.0 / 18.0] * 6 + [1.0 / 36.0] * 12
relax_rate = 1.25


def padded(cells, sides, width, closed):
    for axis, dim in sides:
        count = lax.axis_size(axis)
        ends = count if closed else count - 1
        head = lax.slice_in_dim(cells, 0, width, axis=dim)
        tail = lax.slice_in_dim(cells, cells.shape[dim] - width, cells.shape[dim], axis=dim)
        cells = jnp.concatenate(
            [
                lax.ppermute(tail, axis, [(i, (i + 1) % count) for i in range(ends)]),
                cells,
                lax.ppermute(head, axis, [((i + 1) % count, i) for i in range(ends)]),
            ],
            axis=dim,
        )
    return cells


def collide(pops, wet):
    vel = jnp.asarray(VELOCITIES.T.astype(np.float32))
    weights = jnp.asarray(np.array(WEIGHTS, np.float32))
    rho = jnp.sum(pops, axis=0)
    moment = jnp.einsum("dq,qabz->dabz", vel, pops, precision=lax.Precision.HIGHEST)
    speed = moment / rho[None]
    usq = jnp.sum(speed * speed, axis=0)
    proj = jnp.einsum("dq,dabz->qabz", vel, speed, precision=lax.Precision.HIGHEST)
    feq = (
        weights[:, None, None, None]
        * rho[None]
        * (1.0 + 3.0 * proj + 4.5 * proj * proj - 1.5 * usq[None])
    )
    return jnp.where(wet[None], pops + relax_rate * (feq - pops), pops)


def stream(post, wet):
    sizea, sizeb = (post.shape[1], post.shape[2])
    here = wet[1:-1, 1:-1]
    result = []
    for q in range(19):
        cx, cy, cz = (int(VELOCITIES[q, 0]), int(VELOCITIES[q, 1]), int(VELOCITIES[q, 2]))
        source = jnp.roll(post[q, 1 - cx : sizea - 1 - cx, 1 - cy : sizeb - 1 - cy], cz, axis=-1)
        source_wet = jnp.roll(wet[1 - cx : sizea - 1 - cx, 1 - cy : sizeb - 1 - cy], cz, axis=-1)
        bounced = post[OPPOSITE[q], 1:-1, 1:-1]
        result.append(jnp.where(here, jnp.where(source_wet, source, bounced), post[q, 1:-1, 1:-1]))
    return jnp.stack(result)


def lattice_step(pops, wet):
    return stream(collide(pops, wet), wet)


def per_device(populations, fluid):
    marks = fluid.astype(jnp.float32)[None]
    stacked = jnp.concatenate([populations, marks], axis=0)
    streamwise = padded(stacked, (("gx", 1),), STEPS, True)
    extended = padded(streamwise, (("gy", 2),), STEPS, False)
    current = extended[:19]
    wet = extended[19] > 0.5
    for step in range(STEPS):
        current = lattice_step(current, wet)
        wet = wet[1:-1, 1:-1]
    return current


def solution(mesh):
    return jax.shard_map(
        per_device,
        mesh=mesh,
        in_specs=(P(None, "gx", "gy", None), P("gx", "gy", None)),
        out_specs=P(None, "gx", "gy", None),
        check_vma=False,
    )
```

profile of v0, /device:TPU:2, one launch (start us, length us, event | category | flops | bytes accessed | tf_op | source)
XLA Modules:
  0.0 73.9 jit_solution(5497021437487830090)
XLA Ops:
  0.0 0.7 convert_bitcast_fusion
  0.7 1.0 %pad_maximum_fusion.6 = f32[20,4,8,128]{3,2,1,0:T(8,128)S(1)} fusion(f32[1,4,8,128]{3,2,1,0:T(8,128)S(1)} %convert_bitcast_fusion, f32[19,4,8,128]{3,2,1,0:T(8,128)} %param.10), kind=kLoop, calls=%fused_computation.52 | loop fusion | flops 81920 | bytes 655360 | tf_op jit(solution)/shard_map/concatenate | solution.py:90
  1.7 2.1 %collective-permute-start = (f32[20,4,8,128]{3,2,1,0:T(8,128)S(1)}, f32[20,4,8,128]{3,2,1,0:T(8,128)S(1)}, u32[]{:S(2)}, u32[]{:S(2)}) collective-permute-start(f32[20,4,8,128]{3,2,1,0:T(8,128)S(1)} %pad_maximum_fusion.6), channel_id=1, source_target_pairs={{0,4},{4,8},{8,12},{12,16},{16,20},{20,24},{24,28},{28,32},{32,36}... | collective-permute-start | bytes 983048 | tf_op jit(solution)/shard_map/ppermute | solution.py:46
  3.8 20.6 %collective-permute-start.1 = (f32[20,4,8,128]{3,2,1,0:T(8,128)S(1)}, f32[20,4,8,128]{3,2,1,0:T(8,128)S(1)}, u32[]{:S(2)}, u32[]{:S(2)}) collective-permute-start(f32[20,4,8,128]{3,2,1,0:T(8,128)S(1)} %pad_maximum_fusion.6), channel_id=1, source_target_pairs={{4,0},{8,4},{12,8},{16,12},{20,16},{24,20},{28,24},{32,28},{36,32}... | collective-permute-start | bytes 983048 | tf_op jit(solution)/shard_map/ppermute | solution.py:48
  24.4 2.8 %collective-permute-done = f32[20,4,8,128]{3,2,1,0:T(8,128)S(1)} collective-permute-done((f32[20,4,8,128]{3,2,1,0:T(8,128)S(1)}, f32[20,4,8,128]{3,2,1,0:T(8,128)S(1)}, u32[]{:S(2)}, u32[]{:S(2)}) %collective-permute-start) | collective-permute-done | bytes 327712 | tf_op jit(solution)/shard_map/ppermute | solution.py:46
  27.2 1.8 %collective-permute-done.1 = f32[20,4,8,128]{3,2,1,0:T(8,128)S(1)} collective-permute-done((f32[20,4,8,128]{3,2,1,0:T(8,128)S(1)}, f32[20,4,8,128]{3,2,1,0:T(8,128)S(1)}, u32[]{:S(2)}, u32[]{:S(2)}) %collective-permute-start.1) | collective-permute-done | bytes 327712 | tf_op jit(solution)/shard_map/ppermute | solution.py:48
  28.9 1.0 %pad_maximum_fusion.5 = f32[20,12,8,128]{3,2,1,0:T(8,128)S(1)} fusion(f32[20,4,8,128]{3,2,1,0:T(8,128)S(1)} %collective-permute-done.1, f32[1,4,8,128]{3,2,1,0:T(8,128)S(1)} %convert_bitcast_fusion, f32[19,4,8,128]{3,2,1,0:T(8,128)} %param.10, f32[20,4,8,128]{3,2,1,0:T(8,128)S(1)} %collective-permute-done), kind=kLoop, calls=%fused_computation.42 | loop fusion | flops 737280 | bytes 1966080 | tf_op jit(solution)/shard_map/concatenate | solution.py:44
  30.1 3.4 %collective-permute-start.2 = (f32[20,12,4,128]{3,2,1,0:T(4,128)S(1)}, f32[20,12,4,128]{3,2,1,0:T(4,128)S(1)}, u32[]{:S(2)}, u32[]{:S(2)}) collective-permute-start(f32[20,12,4,128]{3,2,1,0:T(4,128)S(1)} %get-tuple-element.121), channel_id=1, source_target_pairs={{0,1},{1,2},{2,3},{4,5},{5,6},{6,7},{8,9},{9,10},{10,11},{12,13},{... | collective-permute-start | bytes 1474568 | tf_op jit(solution)/shard_map/ppermute | solution.py:46
  33.6 2.5 %collective-permute-start.3 = (f32[20,12,4,128]{3,2,1,0:T(4,128)S(1)}, f32[20,12,4,128]{3,2,1,0:T(4,128)S(1)}, u32[]{:S(2)}, u32[]{:S(2)}) collective-permute-start(f32[20,12,4,128]{3,2,1,0:T(4,128)S(1)} %get-tuple-element.122), channel_id=1, source_target_pairs={{1,0},{2,1},{3,2},{5,4},{6,5},{7,6},{9,8},{10,9},{11,10},{13,12},{... | collective-permute-start | bytes 1474568 | tf_op jit(solution)/shard_map/ppermute | solution.py:48
  36.0 4.8 %collective-permute-done.2 = f32[20,12,4,128]{3,2,1,0:T(4,128)S(1)} collective-permute-done((f32[20,12,4,128]{3,2,1,0:T(4,128)S(1)}, f32[20,12,4,128]{3,2,1,0:T(4,128)S(1)}, u32[]{:S(2)}, u32[]{:S(2)}) %collective-permute-start.2) | collective-permute-done | bytes 491552 | tf_op jit(solution)/shard_map/ppermute | solution.py:46
  40.9 3.4 %collective-permute-done.3 = f32[20,12,4,128]{3,2,1,0:T(4,128)S(1)} collective-permute-done((f32[20,12,4,128]{3,2,1,0:T(4,128)S(1)}, f32[20,12,4,128]{3,2,1,0:T(4,128)S(1)}, u32[]{:S(2)}, u32[]{:S(2)}) %collective-permute-start.3) | collective-permute-done | bytes 491552 | tf_op jit(solution)/shard_map/ppermute | solution.py:48
  44.3 0.4 fusion.295
  44.7 2.9 %multiply_reduce_fusion = (f32[12,16,128]{2,1,0:T(8,128)S(1)}, f32[3,12,16,128]{3,0,2,1:T(4,128)S(1)}) fusion(f32[12,16,128]{2,1,0:T(8,128)S(1)} %get-tuple-element.62, f32[3,19,1,1]{1,0,3,2:T(4,128)S(1)} %copy-done.1, f32[19,12,16,128]{3,2,1,0:T(8,128)S(1)} %get-tuple-element.63), kind=kOutput, calls=%fused_computation.51 | convolution fusion | flops 17006592 | bytes 2359524 | tf_op jit(solution)/shard_map/dq,qabz->dabz/dot_general | solution.py:59
  47.7 0.6 copy-done.2
  48.3 4.0 %add_select_fusion = f32[19,12,16,128]{3,0,2,1:T(8,128)S(1)} fusion(f32[19,12,16,128]{3,2,1,0:T(8,128)S(1)} %get-tuple-element.63, f32[12,16,128]{2,1,0:T(8,128)S(1)} %broadcast_multiply_fusion, f32[12,16,128]{2,1,0:T(8,128)S(1)} %get-tuple-element.62, f32[19]{0:T(128)S(1)} %copy-done.2, pred[12,16,128]{2,1,0:T(8,128)(4,1)S(1)} %fusion.46, ...), kind=kOutput, calls=%fused_computation | convolution fusion | flops 22413312 | bytes 4251952 | tf_op jit(solution)/shard_map/dq,dabz->qabz/dot_general | solution.py:62
  52.3 0.8 %fusion.297 = (f32[1,10,14,128]{3,0,2,1:T(1,128)S(1)}, f32[1,10,14,128]{3,0,2,1:T(1,128)S(1)}, f32[1,10,14,128]{3,0,2,1:T(1,128)S(1)}, f32[1,10,14,128]{3,0,2,1:...) fusion(f32[19,12,16,128]{3,0,2,1:T(8,128)S(1)} %add_select_fusion), kind=kLoop, calls=%fused_computation.514 | loop fusion | bytes 2293760 | tf_op jit(solution)/shard_map/slice | solution.py:77
  53.1 0.9 %fusion.296 = (f32[1,10,14,128]{3,0,2,1:T(1,128)S(1)}, f32[1,10,14,128]{3,0,2,1:T(1,128)S(1)}, f32[1,10,14,128]{3,0,2,1:T(1,128)S(1)}, f32[1,10,14,128]{3,0,2,1:...) fusion(f32[19,12,16,128]{3,0,2,1:T(8,128)S(1)} %add_select_fusion), kind=kLoop, calls=%fused_computation.513 | loop fusion | bytes 2723840 | tf_op jit(solution)/shard_map/slice | solution.py:77
  54.0 0.2 fusion.305
  56.2 0.9 %fusion.108 = (f32[10,14,128]{2,1,0:T(8,128)S(1)}, f32[1,10,14,128]{3,2,1,0:T(8,128)S(1)}, f32[1,10,14,128]{3,2,1,0:T(8,128)S(1)}, f32[1,10,14,128]{3,2,1,0:T(8,...) fusion(f32[1,10,14,128]{3,0,2,1:T(1,128)S(1)} %get-tuple-elemen, ...), kind=kLoop, calls=%fused_computation.240 | loop fusion | flops 1326080 | bytes 4354560 | tf_op jit(solution)/shard_map/mul | solution.py:64
  57.4 2.3 %multiply_reduce_fusion.1 = (f32[10,14,128]{2,1,0:T(8,128)S(1)}, f32[3,10,14,128]{3,0,2,1:T(4,128)S(1)}) fusion(f32[10,14,128]{2,1,0:T(8,128)S(1)} %get-tuple-element.43, f32[3,19,1,1]{1,0,3,2:T(4,128)S(1)} %copy-done.1, f32[19,10,14,128]{3,2,1,0:T(8,128)S(1)} %constant_dynamic-update-slice_fusion), kind=kOutput, calls=%fused_computation.53 | convolution fusion | flops 12400640 | bytes 1720548 | tf_op jit(solution)/shard_map/dq,qabz->dabz/dot_general | solution.py:59
  59.7 1.6 %fusion.307 = f32[19,10,14,128]{3,0,2,1:T(8,128)S(1)} fusion(f32[3,19,1,1]{1,0,3,2:T(4,128)S(1)} %copy-done.1, f32[3,10,14,128]{3,0,2,1:T(4,128)S(1)} %get-tuple-element.218), kind=kOutput, calls=%fused_computation.524 | convolution fusion | flops 12257280 | bytes 1577188 | tf_op jit(solution)/shard_map/dq,dabz->qabz/dot_general | solution.py:62
  61.4 0.7 add_select_fusion.1
  63.0 0.7 add_bitcast_fusion
  63.9 1.4 %multiply_reduce_fusion.2 = (f32[8,12,128]{2,1,0:T(8,128)S(1)}, f32[3,8,12,128]{3,0,2,1:T(4,128)S(1)}) fusion(f32[8,12,128]{2,1,0:T(8,128)S(1)} %get-tuple-element.24, f32[3,19,1,1]{1,0,3,2:T(4,128)S(1)} %copy-done.1, f32[19,8,12,128]{3,2,1,0:T(8,128)S(1)} %constant_dynamic-update-slice_fusion.19), kind=kOutput, calls=%fused_computation.54 | convolution fusion | flops 8503296 | bytes 1179876 | tf_op jit(solution)/shard_map/dq,qabz->dabz/dot_general | solution.py:59
  65.3 1.2 %fusion.308 = f32[19,8,12,128]{3,0,2,1:T(8,128)S(1)} fusion(f32[3,19,1,1]{1,0,3,2:T(4,128)S(1)} %copy-done.1, f32[3,8,12,128]{3,0,2,1:T(4,128)S(1)} %get-tuple-element.220), kind=kOutput, calls=%fused_computation.525 | convolution fusion | flops 8404992 | bytes 1081572 | tf_op jit(solution)/shard_map/dq,dabz->qabz/dot_general | solution.py:62
  66.5 0.5 add_select_fusion.2
  67.9 0.5 add_bitcast_fusion.1
  68.7 0.9 %multiply_reduce_fusion.3 = (f32[6,10,128]{2,1,0:T(8,128)S(1)}, f32[3,6,10,128]{3,0,2,1:T(4,128)S(1)}) fusion(f32[6,10,128]{2,1,0:T(8,128)S(1)} %get-tuple-element.5, f32[3,19,1,1]{1,0,3,2:T(4,128)S(1)} %copy-done.1, f32[19,6,10,128]{3,2,1,0:T(8,128)S(1)} %constant_dynamic-update-slice_fusion.38), kind=kOutput, calls=%fused_computation.131 | convolution fusion | flops 5314560 | bytes 737508 | tf_op jit(solution)/shard_map/dq,qabz->dabz/dot_general | solution.py:59
  69.6 0.8 %fusion.309 = f32[19,6,10,128]{3,0,2,1:T(8,128)S(1)} fusion(f32[3,19,1,1]{1,0,3,2:T(4,128)S(1)} %copy-done.1, f32[3,6,10,128]{3,0,2,1:T(4,128)S(1)} %get-tuple-element.222), kind=kOutput, calls=%fused_computation.526 | convolution fusion | flops 5253120 | bytes 676068 | tf_op jit(solution)/shard_map/dq,dabz->qabz/dot_general | solution.py:62
  70.5 0.4 add_select_fusion.3
  72.5 0.7 copy-done.3
  73.2 0.7 constant_dynamic-update-slice_fusion.57
  (143 shorter events, 5.9 us)
Async XLA Ops:
  1.7 42.6 %copy-start = (f32[19,4,8,128]{3,2,1,0:T(8,128)S(1)}, f32[19,4,8,128]{3,2,1,0:T(8,128)}, u32[]{:S(2)}) copy-start(f32[19,4,8,128]{3,2,1,0:T(8,128)} %param.10) | copy-start | bytes 933892
  1.7 25.5 %collective-permute-start = (f32[20,4,8,128]{3,2,1,0:T(8,128)S(1)}, f32[20,4,8,128]{3,2,1,0:T(8,128)S(1)}, u32[]{:S(2)}, u32[]{:S(2)}) collective-permute-start(f32[20,4,8,128]{3,2,1,0:T(8,128)S(1)} %pad_maximum_fusion.6), channel_id=1, source_target_pairs={{0,4},{4,8},{8,12},{12,16},{16,20},{20,24},{24,28},{28,32},{32,36}... | collective-permute-start | bytes 983048 | tf_op jit(solution)/shard_map/ppermute | solution.py:46
  3.8 25.1 %collective-permute-start.1 = (f32[20,4,8,128]{3,2,1,0:T(8,128)S(1)}, f32[20,4,8,128]{3,2,1,0:T(8,128)S(1)}, u32[]{:S(2)}, u32[]{:S(2)}) collective-permute-start(f32[20,4,8,128]{3,2,1,0:T(8,128)S(1)} %pad_maximum_fusion.6), channel_id=1, source_target_pairs={{4,0},{8,4},{12,8},{16,12},{20,16},{24,20},{28,24},{32,28},{36,32}... | collective-permute-start | bytes 983048 | tf_op jit(solution)/shard_map/ppermute | solution.py:48
  30.1 10.7 %collective-permute-start.2 = (f32[20,12,4,128]{3,2,1,0:T(4,128)S(1)}, f32[20,12,4,128]{3,2,1,0:T(4,128)S(1)}, u32[]{:S(2)}, u32[]{:S(2)}) collective-permute-start(f32[20,12,4,128]{3,2,1,0:T(4,128)S(1)} %get-tuple-element.121), channel_id=1, source_target_pairs={{0,1},{1,2},{2,3},{4,5},{5,6},{6,7},{8,9},{9,10},{10,11},{12,13},{... | collective-permute-start | bytes 1474568 | tf_op jit(solution)/shard_map/ppermute | solution.py:46
  33.5 11.1 %copy-start.1 = (f32[3,19,1,1]{1,0,3,2:T(4,128)S(1)}, f32[3,19,1,1]{1,0,3,2:T(4,128)}, u32[]{:S(2)}) copy-start(f32[3,19,1,1]{1,0,3,2:T(4,128)} %constant.4) | copy-start | bytes 688
  33.6 10.7 %collective-permute-start.3 = (f32[20,12,4,128]{3,2,1,0:T(4,128)S(1)}, f32[20,12,4,128]{3,2,1,0:T(4,128)S(1)}, u32[]{:S(2)}, u32[]{:S(2)}) collective-permute-start(f32[20,12,4,128]{3,2,1,0:T(4,128)S(1)} %get-tuple-element.122), channel_id=1, source_target_pairs={{1,0},{2,1},{3,2},{5,4},{6,5},{7,6},{9,8},{10,9},{11,10},{13,12},{... | collective-permute-start | bytes 1474568 | tf_op jit(solution)/shard_map/ppermute | solution.py:48
  47.6 0.7 copy-start.2
  72.5 0.7 copy-start.3
where the time goes:
time: 74.3 us; the launch traced here: 73.9 us
  starting transfers between devices  28.5 us (38%)
  matrix products  15.2 us (20%)
  waiting for transfers between devices  12.8 us (17%)
  other arithmetic  8.38 us (11%)
  local copies, waits for them, and re-layouts  8.14 us (11%)
  between operations  0.93 us (1%)
    ppermute x2, starting transfers between devices, padded(): lax.ppermute(head, axis, [((i + 1) % count, i) for i in range(ends)])  23 us
    ppermute x2, waiting for transfers between devices, padded(): lax.ppermute(tail, axis, [(i, (i + 1) % count) for i in range(ends)])  7.64 us
    dot_general x4, matrix products, collide(): jnp.einsum('dq,qabz->dabz', vel, pops, precision=lax.Precision.HIGHEST)  7.62 us
    dot_general x4, matrix products, collide(): jnp.einsum('dq,dabz->qabz', vel, speed, precision=lax.Precision.HIGHEST)  7.55 us
    ppermute x2, starting transfers between devices, padded(): lax.ppermute(tail, axis, [(i, (i + 1) % count) for i in range(ends)])  5.45 us
    ppermute x2, waiting for transfers between devices, padded(): lax.ppermute(head, axis, [((i + 1) % count, i) for i in range(ends)])  5.17 us
    slice x40, local copies, waits for them, and re-layouts, stream(): jnp.roll(post[q, 1 - cx:sizea - 1 - cx, 1 - cy:sizeb - 1 - cy], cz, axis=-1)  3.2 us
    mul x3, other arithmetic, collide(): weights[:, None, None, None] * rho[None]  2.04 us
  transfers between devices with their start and end apart: 4, of which 4 were waited for; matrix products, arithmetic and copies ran while one was open for 0% of the time, Pallas kernels for 0%

commit v1 on v0

v1 whole, which is shorter than its diff:
```python
import functools

import jax
import jax.numpy as jnp
from jax import lax
from jax.experimental import pallas as pl
from jax.experimental.pallas import tpu as pltpu
from jax.sharding import PartitionSpec as P

MESH = pl.DeviceIdType.MESH
F32 = jnp.float32

VEL = [
    (0, 0, 0), (1, 0, 0), (-1, 0, 0), (0, 1, 0), (0, -1, 0), (0, 0, 1), (0, 0, -1),
    (1, 1, 0), (-1, -1, 0), (1, -1, 0), (-1, 1, 0), (1, 0, 1), (-1, 0, -1), (1, 0, -1), (-1, 0, 1),
    (0, 1, 1), (0, -1, -1), (0, 1, -1), (0, -1, 1),
]
OPP = [0, 2, 1, 4, 3, 6, 5, 8, 7, 10, 9, 12, 11, 14, 13, 16, 15, 18, 17]
OMEGA = 1.25
ORDER = [2, 8, 10, 12, 14, 0, 3, 4, 5, 6, 15, 16, 17, 18, 1, 7, 9, 11, 13]
SLOT = [ORDER.index(q) for q in range(19)]
LEFT, RIGHT = 0, 1
BELOW, ABOVE = 0, 1


def relax(f):
    even = {q: f[q] + f[q + 1] for q in range(1, 19, 2)}
    odd = {q: f[q] - f[q + 1] for q in range(1, 19, 2)}
    rho = (((f[0] + even[1]) + (even[3] + even[5])) + ((even[7] + even[9]) + (even[11] + even[13]))) + (even[15] + even[17])
    jx = (odd[1] + odd[7]) + (odd[9] + odd[11]) + odd[13]
    jy = (odd[3] + odd[7]) + (odd[15] - odd[9]) + odd[17]
    jz = (odd[5] + odd[11]) + (odd[15] - odd[13]) - odd[17]
    inv = 3.0 / rho
    v = (jx * inv, jy * inv, jz * inv)
    base = 1.0 - (v[0] * v[0] + v[1] * v[1] + v[2] * v[2]) * (1.5 / 9.0)
    out = [None] * 19
    keep = 1.0 - OMEGA
    out[0] = f[0] * keep + (rho * (OMEGA / 3.0)) * base
    for first, last, weight in ((1, 7, 1.0 / 18.0), (7, 19, 1.0 / 36.0)):
        scale = rho * (OMEGA * weight)
        level = scale * base
        half = scale * 0.5
        for q in range(first, last, 2):
            proj = None
            for axis in range(3):
                c = VEL[q][axis]
                if c:
                    term = v[axis]
                    if proj is None:
                        proj = term
                    else:
                        proj = proj + term if c > 0 else proj - term
            sym = level + half * (proj * proj)
            anti = scale * proj
            out[q] = f[q] * keep + (sym + anti)
            out[q + 1] = f[q + 1] * keep + (sym - anti)
    return out


def pulled(grid, masks, level, col, start):
    f = []
    for q in range(19):
        cx, cy, cz = VEL[q]
        src = grid[level, col - cx, SLOT[q], pl.ds(start - cy, 8), :]
        if q == 0:
            f.append(src)
            continue
        if cz:
            src = pltpu.roll(src, cz % 128, 1)
        open_ = masks[col, q - 1, pl.ds(start, 8), :] > 0.5
        f.append(jnp.where(open_, src, grid[level, col, SLOT[OPP[q]], pl.ds(start, 8), :]))
    return f


def column_step(grid, masks, level, col):
    for start in (1, 7):
        post = relax(pulled(grid, masks, level, col, start))
        for q in range(19):
            grid[level + 1, col, SLOT[q], pl.ds(start, 8), :] = post[q]


def mask_column(marks, masks, col):
    for start in (1, 7):
        for q in range(1, 19):
            cx, cy, cz = VEL[q]
            wet = marks[col - cx, pl.ds(start - cy, 8), :]
            if cz:
                wet = pltpu.roll(wet, cz % 128, 1)
            masks[col, q - 1, pl.ds(start, 8), :] = wet


def kernel(nx, ny, zs, pop_ref, fluid_ref, out_ref, f0, wet_in, xs, ms, xr, mxr, yr, myr, cr, mcr, grid, marks, masks,
           load_sem, send_sem, recv_sem):
    gx, gy = lax.axis_index("gx"), lax.axis_index("gy")
    right, left = lax.rem(gx + 1, nx), lax.rem(gx + nx - 1, nx)
    has = (gy > 0, gy < ny - 1)
    seam = lax.rem(gx, zs) == 0

    load_fluid = pltpu.make_async_copy(fluid_ref, wet_in, load_sem.at[4])
    load_fluid.start()
    loads = [pltpu.make_async_copy(pop_ref.at[:, c], f0.at[:, c], load_sem.at[c]) for c in range(4)]
    for c in (3, 2, 1, 0):
        loads[c].start()

    barrier = pltpu.get_barrier_semaphore()
    pl.semaphore_signal(barrier, inc=1, device_id=(left, gy), device_id_type=MESH)
    for d, step in ((BELOW, -1), (ABOVE, 1)):
        @pl.when(has[d])
        def _():
            pl.semaphore_signal(barrier, inc=1, device_id=(gx, gy + step), device_id_type=MESH)

    def copy(number, src, dst, device):
        return pltpu.make_async_remote_copy(
            src_ref=src, dst_ref=dst, send_sem=send_sem.at[number], recv_sem=recv_sem.at[number],
            device_id=device, device_id_type=MESH)

    def to_x(side, k):
        device = (right, gy) if side == LEFT else (left, gy)
        number = side * 5 + k
        if k == 0:
            return copy(number, ms, mxr.at[side], device)
        c = 4 - k if side == LEFT else k - 1
        if k < 4:
            return copy(number, xs.at[c], xr.at[side, k - 1], device)
        part = pl.ds(14, 5) if side == LEFT else pl.ds(0, 5)
        return copy(number, xs.at[c, :, part], xr.at[side, k - 1, :, part], device)

    def to_y(d, k):
        device = (gx, gy + 1) if d == BELOW else (gx, gy - 1)
        h = 1 - d
        number = 10 + 2 * d + k
        if k == 0:
            return copy(number, ms.at[:, h], myr.at[d], device)
        return copy(number, xs.at[:, h], yr.at[d], device)

    def to_corner(d, side, k):
        device = (gx, gy + 1) if d == BELOW else (gx, gy - 1)
        h = 1 - d
        number = 14 + (d * 2 + side) * 5 + k
        if k == 0:
            return copy(number, mxr.at[side, :, h], mcr.at[d, side], device)
        if k < 4:
            return copy(number, xr.at[side, k - 1, h], cr.at[d, side, k - 1], device)
        part = pl.ds(14, 5) if side == LEFT else pl.ds(0, 5)
        return copy(number, xr.at[side, k - 1, h, part], cr.at[d, side, k - 1, part], device)

    def start_y(make):
        for d in (BELOW, ABOVE):
            @pl.when(has[1 - d])
            def _():
                make(d).start()

    def wait_y(make):
        for d in (BELOW, ABOVE):
            @pl.when(has[d])
            def _():
                make(d).wait_recv()

    for d in (BELOW, ABOVE):
        @pl.when(jnp.logical_not(has[d]))
        def _():
            myr[d] = jnp.zeros((4, 4, 128), F32)
            mcr[d] = jnp.zeros((2, 4, 4, 128), F32)

    load_fluid.wait()
    for c in range(4):
        wet = wet_in[c].astype(F32)
        marks[4 + c, pl.ds(4, 8), :] = wet
        ms[c, 0] = wet[0:4]
        ms[c, 1] = wet[4:8]

    def own(c):
        loads[c].wait()
        post = relax([f0[q, c] for q in range(19)])
        for q in range(19):
            xs[c, 0, SLOT[q]] = post[q][0:4]
            xs[c, 1, SLOT[q]] = post[q][4:8]
            grid[0, 4 + c, SLOT[q], pl.ds(4, 8), :] = post[q]

    own(3)
    pl.semaphore_wait(barrier, 1 + (gy + ny - 1) // ny + (2 * ny - 2 - gy) // ny)
    to_x(LEFT, 0).start()
    to_x(LEFT, 1).start()
    for c in (2, 1, 0):
        own(c)
        to_x(LEFT, 4 - c).start()
    start_y(lambda d: to_y(d, 0))
    start_y(lambda d: to_y(d, 1))

    def meet_left():
        to_x(LEFT, 0).wait_recv()
        for k in range(5):
            to_x(RIGHT, k).start()
        start_y(lambda d: to_corner(d, LEFT, 0))

    @pl.when(jnp.logical_not(seam))
    def _():
        meet_left()

    def unpack_marks(side):
        for c in range(4):
            col = c if side == LEFT else 8 + c
            marks[col, pl.ds(4, 4), :] = mxr[side, c, 0]
            marks[col, pl.ds(8, 4), :] = mxr[side, c, 1]
            marks[col, pl.ds(0, 4), :] = mcr[BELOW, side, c]
            marks[col, pl.ds(12, 4), :] = mcr[ABOVE, side, c]

    def unpack(side, k):
        c = 4 - k if side == LEFT else 8 + k - 1
        slots = range(19) if k < 4 else (range(14, 19) if side == LEFT else range(5))
        for s in slots:
            grid[0, c, s, pl.ds(4, 4), :] = xr[side, k - 1, 0, s]
            grid[0, c, s, pl.ds(8, 4), :] = xr[side, k - 1, 1, s]
            grid[0, c, s, pl.ds(0, 4), :] = cr[BELOW, side, k - 1, s]
            grid[0, c, s, pl.ds(12, 4), :] = cr[ABOVE, side, k - 1, s]

    wait_y(lambda d: to_y(d, 0))
    for c in range(4):
        marks[4 + c, pl.ds(0, 4), :] = myr[BELOW, c]
        marks[4 + c, pl.ds(12, 4), :] = myr[ABOVE, c]
    to_x(RIGHT, 0).wait_recv()
    start_y(lambda d: to_corner(d, RIGHT, 0))
    for k in range(1, 5):
        to_x(RIGHT, k).wait_recv()
        start_y(lambda d: to_corner(d, RIGHT, k))
    wait_y(lambda d: to_y(d, 1))

    def fill_rows(c, carry):
        for s in range(19):
            grid[0, 4 + c, s, pl.ds(0, 4), :] = yr[BELOW, c, s]
            grid[0, 4 + c, s, pl.ds(12, 4), :] = yr[ABOVE, c, s]
        return carry

    lax.fori_loop(0, 4, fill_rows, 0)
    wait_y(lambda d: to_corner(d, RIGHT, 0))
    unpack_marks(RIGHT)

    def mask_range(low, high):
        def body(col, carry):
            mask_column(marks, masks, col)
            return carry
        lax.fori_loop(low, high, body, 0)

    mask_range(5, 11)
    for k in range(1, 5):
        wait_y(lambda d: to_corner(d, RIGHT, k))
        unpack(RIGHT, k)

    for level, low, high in ((0, 5, 11), (1, 6, 10), (2, 7, 9)):
        def body(col, carry, level=level):
            column_step(grid, masks, level, col)
            return carry
        lax.fori_loop(low, high, body, 0)

    @pl.when(seam)
    def _():
        meet_left()

    for k in range(1, 5):
        to_x(LEFT, k).wait_recv()
        start_y(lambda d: to_corner(d, LEFT, k))
    wait_y(lambda d: to_corner(d, LEFT, 0))
    unpack_marks(LEFT)
    mask_range(1, 5)
    for k in range(1, 5):
        wait_y(lambda d: to_corner(d, LEFT, k))
        unpack(LEFT, k)

        def body(level, carry, k=k):
            column_step(grid, masks, level, level + 5 - k)
            return carry

        lax.fori_loop(0, 3, body, 0)
        c = 4 - k
        f = pulled(grid, masks, 3, 4 + c, 4)
        wet = wet_in[c] == 1
        for q in range(19):
            out_ref[q, c] = jnp.where(wet, f[q], f0[q, c])

    for side in (LEFT, RIGHT):
        for k in range(5):
            to_x(side, k).wait_send()
    for d in (BELOW, ABOVE):
        @pl.when(has[1 - d])
        def _():
            for k in range(2):
                to_y(d, k).wait_send()
            for side in (LEFT, RIGHT):
                for k in range(5):
                    to_corner(d, side, k).wait_send()


def per_device(nx, ny, zs, populations, fluid):
    hbm = pl.BlockSpec(memory_space=pltpu.HBM)
    vm = lambda *shape: pltpu.VMEM(shape, F32)
    return pl.pallas_call(
        functools.partial(kernel, nx, ny, zs),
        out_shape=pltpu.VMEM(populations.shape, F32),
        in_specs=[hbm, hbm],
        out_specs=pl.BlockSpec(memory_space=pltpu.VMEM),
        scratch_shapes=[
            vm(19, 4, 8, 128),
            pltpu.VMEM((4, 8, 128), jnp.int32),
            vm(4, 2, 19, 4, 128),
            vm(4, 2, 4, 128),
            vm(2, 4, 2, 19, 4, 128),
            vm(2, 4, 2, 4, 128),
            vm(2, 4, 19, 4, 128),
            vm(2, 4, 4, 128),
            vm(2, 2, 4, 19, 4, 128),
            vm(2, 2, 4, 4, 128),
            vm(4, 12, 19, 16, 128),
            vm(12, 16, 128),
            vm(12, 18, 16, 128),
            pltpu.SemaphoreType.DMA((5,)),
            pltpu.SemaphoreType.DMA((34,)),
            pltpu.SemaphoreType.DMA((34,)),
        ],
        compiler_params=pltpu.CompilerParams(
            collective_id=0, has_side_effects=True, vmem_limit_bytes=32 * 2**20
        ),
    )(*(pltpu.with_memory_space_constraint(a, pltpu.HBM) for a in (populations, fluid)))


def solution(mesh):
    nx, ny = mesh.shape["gx"], mesh.shape["gy"]
    return jax.shard_map(
        functools.partial(per_device, nx, ny, min(nx, 32)),
        mesh=mesh,
        in_specs=(P(None, "gx", "gy", None), P("gx", "gy", None)),
        out_specs=P(None, "gx", "gy", None),
        check_vma=False,
    )
```

time: 74.3 us -> 30.6 us (0.41)
  Pallas kernels: 0 us -> 29.7 us
  starting transfers between devices: 28.5 us -> 0 us
  matrix products: 15.2 us -> 0 us
  waiting for transfers between devices: 12.8 us -> 0 us
  other arithmetic: 8.38 us -> 0 us
  local copies, waits for them, and re-layouts: 8.14 us -> 0.72 us
  between operations: 0.93 us -> 0.01 us
    pallas_call x0 -> x1, Pallas kernels: none -> 29.7 us  [per_device(): pl.pallas_call(functools.partial(kernel, nx, ny, zs), out_shape=pltpu.VME...]
    ppermute x4 -> x0, starting transfers between devices: 28.5 us -> none  [the longest x2 23 us: padded(): lax.ppermute(head, axis, [((i + 1) % count, i) for i in range(ends)])]
    dot_general x8 -> x0, matrix products: 15.2 us -> none  [the longest x4 7.62 us: collide(): jnp.einsum('dq,qabz->dabz', vel, pops, precision=lax.Precision.HIGHEST)]
    ppermute x4 -> x0, waiting for transfers between devices: 12.8 us -> none  [the longest x2 7.64 us: padded(): lax.ppermute(tail, axis, [(i, (i + 1) % count) for i in range(ends)])]
    slice x54 -> x0, local copies, waits for them, and re-layouts: 6.22 us -> none  [the longest x40 3.2 us: stream(): jnp.roll(post[q, 1 - cx:sizea - 1 - cx, 1 - cy:sizeb - 1 - cy], cz, axis=-1)]
    mul x7 -> x0, other arithmetic: 2.07 us -> none  [the longest x3 2.04 us: collide(): weights[:, None, None, None] * rho[None]]
    concatenate x2 -> x0, other arithmetic: 2.02 us -> none  [the longest x1 1.03 us: padded(): jnp.concatenate([lax.ppermute(tail, axis, [(i, (i + 1) % count) for i in...]
    select_n x3 -> x0, other arithmetic: 1.62 us -> none  [collide(): return jnp.where(wet[None], pops + relax_rate * (feq - pops), pops)]
  transfers between devices with their start and end apart: 4 -> 0, of which waited for: 4 -> 0; matrix products, arithmetic and copies ran while one was open for 0% -> 0% of each run, Pallas kernels for 0% -> 0%
where the time goes in v1:
time: 30.6 us; the launch traced here: 30.4 us
  Pallas kernels  29.7 us (97%)
  local copies, waits for them, and re-layouts  0.72 us (2%)
    pallas_call x1, Pallas kernels, per_device(): pl.pallas_call(functools.partial(kernel, nx, ny, zs), out_shape=pltpu.VME...  29.7 us
    unnamed x1, local copies, waits for them, and re-layouts  0.72 us

profile of v1, /device:TPU:2, one launch (start us, length us, event | category | flops | bytes accessed | tf_op | source)
XLA Modules:
  0.0 30.4 jit_solution(1181077210187011018)
XLA Ops:
  0.0 29.7 %shard_map.28 = f32[19,4,8,128]{3,2,1,0:T(8,128)S(1)} custom-call(f32[19,4,8,128]{3,2,1,0:T(8,128)} %pop_ref.1, s32[4,8,128]{2,1,0:T(8,128)} %fluid_ref.1), custom_call_target="tpu_custom_call" | custom-call | tf_op jit(solution)/shard_map/pallas_call | solution.py:296
  29.7 0.7 %copy.4 = f32[19,4,8,128]{3,2,1,0:T(8,128)} copy(f32[19,4,8,128]{3,2,1,0:T(8,128)S(1)} %shard_map.28) | data formatting | bytes 622592

commit v2 on v1

v2 whole, which is shorter than its diff:
```python
import functools

import jax
import jax.numpy as jnp
from jax import lax
from jax.experimental import pallas as pl
from jax.experimental.pallas import tpu as pltpu
from jax.sharding import PartitionSpec as P

MESH = pl.DeviceIdType.MESH
F32 = jnp.float32

VEL = [
    (0, 0, 0), (1, 0, 0), (-1, 0, 0), (0, 1, 0), (0, -1, 0), (0, 0, 1), (0, 0, -1),
    (1, 1, 0), (-1, -1, 0), (1, -1, 0), (-1, 1, 0), (1, 0, 1), (-1, 0, -1), (1, 0, -1), (-1, 0, 1),
    (0, 1, 1), (0, -1, -1), (0, 1, -1), (0, -1, 1),
]
OPP = [0, 2, 1, 4, 3, 6, 5, 8, 7, 10, 9, 12, 11, 14, 13, 16, 15, 18, 17]
OMEGA = 1.25
ORDER = [2, 8, 10, 12, 14, 0, 3, 4, 5, 6, 15, 16, 17, 18, 1, 7, 9, 11, 13]
SLOT = [ORDER.index(q) for q in range(19)]
LEFT, RIGHT = 0, 1
BELOW, ABOVE = 0, 1


def relax(f):
    even = {q: f[q] + f[q + 1] for q in range(1, 19, 2)}
    odd = {q: f[q] - f[q + 1] for q in range(1, 19, 2)}
    rho = (((f[0] + even[1]) + (even[3] + even[5])) + ((even[7] + even[9]) + (even[11] + even[13]))) + (even[15] + even[17])
    jx = (odd[1] + odd[7]) + (odd[9] + odd[11]) + odd[13]
    jy = (odd[3] + odd[7]) + (odd[15] - odd[9]) + odd[17]
    jz = (odd[5] + odd[11]) + (odd[15] - odd[13]) - odd[17]
    inv = 3.0 / rho
    v = (jx * inv, jy * inv, jz * inv)
    base = 1.0 - (v[0] * v[0] + v[1] * v[1] + v[2] * v[2]) * (1.5 / 9.0)
    out = [None] * 19
    keep = 1.0 - OMEGA
    out[0] = f[0] * keep + (rho * (OMEGA / 3.0)) * base
    for first, last, weight in ((1, 7, 1.0 / 18.0), (7, 19, 1.0 / 36.0)):
        scale = rho * (OMEGA * weight)
        level = scale * base
        half = scale * 0.5
        for q in range(first, last, 2):
            proj = None
            for axis in range(3):
                c = VEL[q][axis]
                if c:
                    term = v[axis]
                    if proj is None:
                        proj = term
                    else:
                        proj = proj + term if c > 0 else proj - term
            sym = level + half * (proj * proj)
            anti = scale * proj
            out[q] = f[q] * keep + (sym + anti)
            out[q + 1] = f[q + 1] * keep + (sym - anti)
    return out


def pulled(grid, masks, level, col, start):
    f = []
    for q in range(19):
        cx, cy, cz = VEL[q]
        src = grid[level, col - cx, SLOT[q], pl.ds(start - cy, 8), :]
        if q == 0:
            f.append(src)
            continue
        if cz:
            src = pltpu.roll(src, cz % 128, 1)
        open_ = masks[col, q - 1, pl.ds(start, 8), :] > 0.5
        f.append(jnp.where(open_, src, grid[level, col, SLOT[OPP[q]], pl.ds(start, 8), :]))
    return f


def column_steps(grid, masks, level, cols):
    for col in cols:
        for start in (1, 7):
            post = relax(pulled(grid, masks, level, col, start))
            for q in range(19):
                grid[level + 1, col, SLOT[q], pl.ds(start, 8), :] = post[q]


def mask_columns(marks, masks, cols):
    for col in cols:
        for start in (1, 7):
            for q in range(1, 19):
                cx, cy, cz = VEL[q]
                wet = marks[col - cx, pl.ds(start - cy, 8), :]
                if cz:
                    wet = pltpu.roll(wet, cz % 128, 1)
                masks[col, q - 1, pl.ds(start, 8), :] = wet


FROM_LEFT = 0
FROM_RIGHT = 4
FROM_Y = 6
LEFT_CORNER = 8
RIGHT_CORNER = 16
ARRIVALS = 20
TO_X, TO_X_SECOND, TO_ABOVE, TO_BELOW = range(4)
UNITS = {"column": 38, "far": 48, "all": 124, "rows": 80, "corner": 19, "far_corner": 24, "all_corner": 62}


def kernel(nx, ny, zs, pop_ref, fluid_ref, out_ref, f0, wet_in, xs, ms, xr, mxr, yr, myr, cr, mcr, grid, marks, masks, units,
           load_sem, send_sem, recv_sem):
    gx, gy = lax.axis_index("gx"), lax.axis_index("gy")
    right, left = lax.rem(gx + 1, nx), lax.rem(gx + nx - 1, nx)
    has = (gy > 0, gy < ny - 1)
    seam = lax.rem(gx, zs) == 0

    load_fluid = pltpu.make_async_copy(fluid_ref, wet_in, load_sem.at[0])
    load_last = pltpu.make_async_copy(pop_ref.at[:, pl.ds(3, 1)], f0.at[:, pl.ds(3, 1)], load_sem.at[1])
    load_rest = pltpu.make_async_copy(pop_ref.at[:, pl.ds(0, 3)], f0.at[:, pl.ds(0, 3)], load_sem.at[2])
    load_fluid.start()
    load_last.start()
    load_rest.start()

    barrier = pltpu.get_barrier_semaphore()
    pl.semaphore_signal(barrier, inc=1, device_id=(left, gy), device_id_type=MESH)
    for d, step in ((BELOW, -1), (ABOVE, 1)):
        @pl.when(has[d])
        def _():
            pl.semaphore_signal(barrier, inc=1, device_id=(left, gy + step), device_id_type=MESH)
            pl.semaphore_signal(barrier, inc=1, device_id=(gx, gy + step), device_id_type=MESH)

    def copy(src, dst, sent, arrived, device):
        return pltpu.make_async_remote_copy(
            src_ref=src, dst_ref=dst, send_sem=send_sem.at[sent], recv_sem=recv_sem.at[arrived],
            device_id=device, device_id_type=MESH)

    def arrive(number, count):
        part = units.at[pl.ds(0, count)]
        copy(part, part, 0, number, (right, gy)).wait_recv()

    def departed(sent, count):
        part = units.at[pl.ds(0, count)]
        copy(part, part, sent, 0, (right, gy)).wait_send()

    LEFT_PART, RIGHT_PART = pl.ds(14, 5), pl.ds(0, 5)

    def row_of(d):
        return gy + 1 if d == BELOW else gy - 1

    def start_y(make):
        for d in (BELOW, ABOVE):
            @pl.when(has[1 - d])
            def _():
                for one in make(d, 1 - d, TO_ABOVE if d == BELOW else TO_BELOW):
                    one.start()

    def wait_y(number, stride, count):
        for d in (BELOW, ABOVE):
            @pl.when(has[d])
            def _():
                arrive(number + stride * d, count)

    for d in (BELOW, ABOVE):
        @pl.when(jnp.logical_not(has[d]))
        def _():
            myr[d] = jnp.zeros((4, 4, 128), F32)
            mcr[d] = jnp.zeros((2, 4, 4, 128), F32)

    load_fluid.wait()
    for c in range(4):
        wet = wet_in[c].astype(F32)
        marks[4 + c, pl.ds(4, 8), :] = wet
        ms[c, 0] = wet[0:4]
        ms[c, 1] = wet[4:8]

    def own(c):
        post = relax([f0[q, c] for q in range(19)])
        for q in range(19):
            xs[c, 0, SLOT[q]] = post[q][0:4]
            xs[c, 1, SLOT[q]] = post[q][4:8]
            grid[0, 4 + c, SLOT[q], pl.ds(4, 8), :] = post[q]

    load_last.wait()
    own(3)
    pl.semaphore_wait(barrier, 1 + 2 * ((gy + ny - 1) // ny) + 2 * ((2 * ny - 2 - gy) // ny))
    to_right = (right, gy)
    copy(ms, mxr.at[LEFT], TO_X, FROM_LEFT, to_right).start()
    copy(xs.at[3], xr.at[LEFT, 0], TO_X, FROM_LEFT + 1, to_right).start()
    load_rest.wait()
    own(2)
    second = copy(xs.at[2], xr.at[LEFT, 1], TO_X_SECOND, FROM_LEFT + 2, to_right)
    second.start()
    own(1)
    copy(xs.at[1], xr.at[LEFT, 2], TO_X, FROM_LEFT + 3, to_right).start()
    own(0)
    copy(xs.at[0, :, LEFT_PART], xr.at[LEFT, 3, :, LEFT_PART], TO_X, FROM_LEFT + 3, to_right).start()
    start_y(lambda d, h, sent: [copy(ms.at[:, h], myr.at[d], sent, FROM_Y + d, (gx, row_of(d)))])
    second.wait_send()
    start_y(lambda d, h, sent: [
        copy(xs.at[1, h], cr.at[d, LEFT, 2], sent, LEFT_CORNER + 4 * d + 3, (right, row_of(d))),
        copy(xs.at[0, h, LEFT_PART], cr.at[d, LEFT, 3, LEFT_PART], sent, LEFT_CORNER + 4 * d + 3, (right, row_of(d))),
        copy(xs.at[:, h], yr.at[d], sent, FROM_Y + d, (gx, row_of(d))),
    ])

    def meet_left():
        arrive(FROM_LEFT, 8)
        to_left = (left, gy)
        copy(ms, mxr.at[RIGHT], TO_X, FROM_RIGHT, to_left).start()
        copy(xs.at[pl.ds(0, 3)], xr.at[RIGHT, pl.ds(0, 3)], TO_X, FROM_RIGHT + 1, to_left).start()
        copy(xs.at[3, :, RIGHT_PART], xr.at[RIGHT, 3, :, RIGHT_PART], TO_X, FROM_RIGHT + 1, to_left).start()
        start_y(lambda d, h, sent: [
            copy(mxr.at[LEFT, :, h], mcr.at[d, LEFT], sent, LEFT_CORNER + 4 * d, (gx, row_of(d)))])

    @pl.when(jnp.logical_not(seam))
    def _():
        meet_left()

    def unpack_marks(side):
        for c in range(4):
            col = c if side == LEFT else 8 + c
            marks[col, pl.ds(4, 4), :] = mxr[side, c, 0]
            marks[col, pl.ds(8, 4), :] = mxr[side, c, 1]
            marks[col, pl.ds(0, 4), :] = mcr[BELOW, side, c]
            marks[col, pl.ds(12, 4), :] = mcr[ABOVE, side, c]

    def unpack(side, k):
        c = 4 - k if side == LEFT else 8 + k - 1
        slots = range(19) if k < 4 else (range(14, 19) if side == LEFT else range(5))
        for s in slots:
            grid[0, c, s, pl.ds(4, 4), :] = xr[side, k - 1, 0, s]
            grid[0, c, s, pl.ds(8, 4), :] = xr[side, k - 1, 1, s]
            grid[0, c, s, pl.ds(0, 4), :] = cr[BELOW, side, k - 1, s]
            grid[0, c, s, pl.ds(12, 4), :] = cr[ABOVE, side, k - 1, s]

    def loop(count, make):
        def body(i, carry):
            make(i)
            return carry
        lax.fori_loop(0, count, body, 0)

    arrive(FROM_RIGHT, 8)
    start_y(lambda d, h, sent: [
        copy(mxr.at[RIGHT, :, h], mcr.at[d, RIGHT], sent, RIGHT_CORNER + 2 * d, (gx, row_of(d)))])
    arrive(FROM_RIGHT + 1, UNITS["all"])
    start_y(lambda d, h, sent: [
        copy(xr.at[RIGHT, pl.ds(0, 3), h], cr.at[d, RIGHT, pl.ds(0, 3)], sent, RIGHT_CORNER + 2 * d + 1, (gx, row_of(d))),
        copy(xr.at[RIGHT, 3, h, RIGHT_PART], cr.at[d, RIGHT, 3, RIGHT_PART], sent, RIGHT_CORNER + 2 * d + 1, (gx, row_of(d))),
    ])
    wait_y(FROM_Y, 1, UNITS["rows"])
    for c in range(4):
        marks[4 + c, pl.ds(0, 4), :] = myr[BELOW, c]
        marks[4 + c, pl.ds(12, 4), :] = myr[ABOVE, c]

    def fill_rows(c):
        for s in range(19):
            grid[0, 4 + c, s, pl.ds(0, 4), :] = yr[BELOW, c, s]
            grid[0, 4 + c, s, pl.ds(12, 4), :] = yr[ABOVE, c, s]

    loop(4, fill_rows)
    wait_y(RIGHT_CORNER, 2, 4)
    unpack_marks(RIGHT)
    loop(3, lambda i: mask_columns(marks, masks, (5 + 2 * i, 6 + 2 * i)))
    wait_y(RIGHT_CORNER + 1, 2, UNITS["all_corner"])
    for k in range(1, 5):
        unpack(RIGHT, k)

    loop(3, lambda i: column_steps(grid, masks, 0, (5 + 2 * i, 6 + 2 * i)))

    @pl.when(seam)
    def _():
        meet_left()

    def pass_on(k):
        arrive(FROM_LEFT + k, UNITS["column"])
        start_y(lambda d, h, sent: [
            copy(xr.at[LEFT, k - 1, h], cr.at[d, LEFT, k - 1], sent, LEFT_CORNER + 4 * d + k, (gx, row_of(d)))])

    pass_on(1)
    loop(2, lambda i: column_steps(grid, masks, 1, (6 + 2 * i, 7 + 2 * i)))
    pass_on(2)
    column_steps(grid, masks, 2, (7, 8))

    wait_y(LEFT_CORNER, 4, 4)
    unpack_marks(LEFT)
    loop(2, lambda i: mask_columns(marks, masks, (1 + 2 * i, 2 + 2 * i)))

    def finish(c):
        f = pulled(grid, masks, 3, 4 + c, 4)
        wet = wet_in[c] == 1
        for q in range(19):
            out_ref[q, c] = jnp.where(wet, f[q], f0[q, c])

    for k in (1, 2):
        wait_y(LEFT_CORNER + k, 4, UNITS["corner"])
        unpack(LEFT, k)
        loop(3, lambda level: column_steps(grid, masks, level, (level + 5 - k,)))
        finish(4 - k)
    arrive(FROM_LEFT + 3, UNITS["far"])
    wait_y(LEFT_CORNER + 3, 4, UNITS["far_corner"])
    unpack(LEFT, 3)
    unpack(LEFT, 4)
    loop(3, lambda level: column_steps(grid, masks, level, (level + 1, level + 2)))
    finish(1)
    finish(0)

    departed(TO_X, 8 + 38 + UNITS["far"] + 8 + UNITS["all"])
    for d in (BELOW, ABOVE):
        @pl.when(has[1 - d])
        def _():
            departed(
                TO_ABOVE if d == BELOW else TO_BELOW,
                UNITS["rows"] + 4 + 2 * UNITS["corner"] + UNITS["far_corner"] + 4 + UNITS["all_corner"])


def per_device(nx, ny, zs, populations, fluid):
    hbm = pl.BlockSpec(memory_space=pltpu.HBM)
    vm = lambda *shape: pltpu.VMEM(shape, F32)
    return pl.pallas_call(
        functools.partial(kernel, nx, ny, zs),
        out_shape=pltpu.VMEM(populations.shape, F32),
        in_specs=[hbm, hbm],
        out_specs=pl.BlockSpec(memory_space=pltpu.VMEM),
        scratch_shapes=[
            vm(19, 4, 8, 128),
            pltpu.VMEM((4, 8, 128), jnp.int32),
            vm(4, 2, 19, 4, 128),
            vm(4, 2, 4, 128),
            vm(2, 4, 2, 19, 4, 128),
            vm(2, 4, 2, 4, 128),
            vm(2, 4, 19, 4, 128),
            vm(2, 4, 4, 128),
            vm(2, 2, 4, 19, 4, 128),
            vm(2, 2, 4, 4, 128),
            vm(4, 12, 19, 16, 128),
            vm(12, 16, 128),
            vm(12, 18, 16, 128),
            vm(256, 4, 128),
            pltpu.SemaphoreType.DMA((3,)),
            pltpu.SemaphoreType.DMA((4,)),
            pltpu.SemaphoreType.DMA((ARRIVALS,)),
        ],
        compiler_params=pltpu.CompilerParams(
            collective_id=0, has_side_effects=True, vmem_limit_bytes=32 * 2**20
        ),
    )(*(pltpu.with_memory_space_constraint(a, pltpu.HBM) for a in (populations, fluid)))


def solution(mesh):
    nx, ny = mesh.shape["gx"], mesh.shape["gy"]
    return jax.shard_map(
        functools.partial(per_device, nx, ny, min(nx, 32)),
        mesh=mesh,
        in_specs=(P(None, "gx", "gy", None), P("gx", "gy", None)),
        out_specs=P(None, "gx", "gy", None),
        check_vma=False,
    )
```

time: 30.6 us -> 29.3 us (0.958)
  Pallas kernels: 29.7 us -> 28.4 us
    pallas_call x1, Pallas kernels: 29.7 us -> 28.4 us  [per_device(): pl.pallas_call(functools.partial(kernel, nx, ny, zs), out_shape=pltpu.VME...]
where the time goes in v2:
time: 29.3 us; the launch traced here: 29.1 us
  Pallas kernels  28.4 us (97%)
  local copies, waits for them, and re-layouts  0.72 us (2%)
    pallas_call x1, Pallas kernels, per_device(): pl.pallas_call(functools.partial(kernel, nx, ny, zs), out_shape=pltpu.VME...  28.4 us
    unnamed x1, local copies, waits for them, and re-layouts  0.72 us

profile of v2, /device:TPU:2, one launch (start us, length us, event | category | flops | bytes accessed | tf_op | source)
XLA Modules:
  0.0 29.1 jit_solution(16319019626366185174)
XLA Ops:
  0.0 28.4 %shard_map.28 = f32[19,4,8,128]{3,2,1,0:T(8,128)S(1)} custom-call(f32[19,4,8,128]{3,2,1,0:T(8,128)} %pop_ref.1, s32[4,8,128]{2,1,0:T(8,128)} %fluid_ref.1), custom_call_target="tpu_custom_call" | custom-call | tf_op jit(solution)/shard_map/pallas_call | solution.py:312
  28.4 0.7 %copy.4 = f32[19,4,8,128]{3,2,1,0:T(8,128)} copy(f32[19,4,8,128]{3,2,1,0:T(8,128)S(1)} %shard_map.28) | data formatting | bytes 622592

commit v3 on v2

--- a/solution.py
+++ b/solution.py
@@ -23,7 +23,7 @@
 BELOW, ABOVE = 0, 1
 
 
-def relax(f):
+def relax(f, wanted=range(19)):
     even = {q: f[q] + f[q + 1] for q in range(1, 19, 2)}
     odd = {q: f[q] - f[q + 1] for q in range(1, 19, 2)}
     rho = (((f[0] + even[1]) + (even[3] + even[5])) + ((even[7] + even[9]) + (even[11] + even[13]))) + (even[15] + even[17])
@@ -35,7 +35,8 @@
     base = 1.0 - (v[0] * v[0] + v[1] * v[1] + v[2] * v[2]) * (1.5 / 9.0)
     out = [None] * 19
     keep = 1.0 - OMEGA
-    out[0] = f[0] * keep + (rho * (OMEGA / 3.0)) * base
+    if 0 in wanted:
+        out[0] = f[0] * keep + (rho * (OMEGA / 3.0)) * base
     for first, last, weight in ((1, 7, 1.0 / 18.0), (7, 19, 1.0 / 36.0)):
         scale = rho * (OMEGA * weight)
         level = scale * base
@@ -52,8 +53,10 @@
                         proj = proj + term if c > 0 else proj - term
             sym = level + half * (proj * proj)
             anti = scale * proj
-            out[q] = f[q] * keep + (sym + anti)
-            out[q + 1] = f[q + 1] * keep + (sym - anti)
+            if q in wanted:
+                out[q] = f[q] * keep + (sym + anti)
+            if q + 1 in wanted:
+                out[q + 1] = f[q + 1] * keep + (sym - anti)
     return out
 
 
@@ -72,11 +75,11 @@
     return f
 
 
-def column_steps(grid, masks, level, cols):
+def column_steps(grid, masks, level, cols, wanted=range(19)):
     for col in cols:
         for start in (1, 7):
-            post = relax(pulled(grid, masks, level, col, start))
-            for q in range(19):
+            post = relax(pulled(grid, masks, level, col, start), wanted)
+            for q in wanted:
                 grid[level + 1, col, SLOT[q], pl.ds(start, 8), :] = post[q]
 
 
@@ -92,11 +95,11 @@
 
 
 FROM_LEFT = 0
-FROM_RIGHT = 4
-FROM_Y = 6
-LEFT_CORNER = 8
-RIGHT_CORNER = 16
-ARRIVALS = 20
+FROM_RIGHT = 6
+FROM_Y = 8
+LEFT_CORNER = 10
+RIGHT_CORNER = 18
+ARRIVALS = 22
 TO_X, TO_X_SECOND, TO_ABOVE, TO_BELOW = range(4)
 UNITS = {"column": 38, "far": 48, "all": 124, "rows": 80, "corner": 19, "far_corner": 24, "all_corner": 62}
 
@@ -108,6 +111,14 @@
     has = (gy > 0, gy < ny - 1)
     seam = lax.rem(gx, zs) == 0
 
+    barrier = pltpu.get_barrier_semaphore()
+    for d, step in ((BELOW, -1), (ABOVE, 1)):
+        @pl.when(has[d])
+        def _():
+            pl.semaphore_signal(barrier, inc=1, device_id=(gx, gy + step), device_id_type=MESH)
+            pl.semaphore_signal(barrier, inc=1, device_id=(left, gy + step), device_id_type=MESH)
+    pl.semaphore_signal(barrier, inc=1, device_id=(left, gy), device_id_type=MESH)
+
     load_fluid = pltpu.make_async_copy(fluid_ref, wet_in, load_sem.at[0])
     load_last = pltpu.make_async_copy(pop_ref.at[:, pl.ds(3, 1)], f0.at[:, pl.ds(3, 1)], load_sem.at[1])
     load_rest = pltpu.make_async_copy(pop_ref.at[:, pl.ds(0, 3)], f0.at[:, pl.ds(0, 3)], load_sem.at[2])
@@ -115,14 +126,6 @@
     load_last.start()
     load_rest.start()
 
-    barrier = pltpu.get_barrier_semaphore()
-    pl.semaphore_signal(barrier, inc=1, device_id=(left, gy), device_id_type=MESH)
-    for d, step in ((BELOW, -1), (ABOVE, 1)):
-        @pl.when(has[d])
-        def _():
-            pl.semaphore_signal(barrier, inc=1, device_id=(left, gy + step), device_id_type=MESH)
-            pl.semaphore_signal(barrier, inc=1, device_id=(gx, gy + step), device_id_type=MESH)
-
     def copy(src, dst, sent, arrived, device):
         return pltpu.make_async_remote_copy(
             src_ref=src, dst_ref=dst, send_sem=send_sem.at[sent], recv_sem=recv_sem.at[arrived],
@@ -178,16 +181,18 @@
     own(3)
     pl.semaphore_wait(barrier, 1 + 2 * ((gy + ny - 1) // ny) + 2 * ((2 * ny - 2 - gy) // ny))
     to_right = (right, gy)
+    copy(xs.at[3, 0], xr.at[LEFT, 0, 0], TO_X, FROM_LEFT + 1, to_right).start()
     copy(ms, mxr.at[LEFT], TO_X, FROM_LEFT, to_right).start()
-    copy(xs.at[3], xr.at[LEFT, 0], TO_X, FROM_LEFT + 1, to_right).start()
+    copy(xs.at[3, 1], xr.at[LEFT, 0, 1], TO_X, FROM_LEFT + 2, to_right).start()
     load_rest.wait()
     own(2)
-    second = copy(xs.at[2], xr.at[LEFT, 1], TO_X_SECOND, FROM_LEFT + 2, to_right)
+    second = copy(xs.at[2, 0], xr.at[LEFT, 1, 0], TO_X_SECOND, FROM_LEFT + 3, to_right)
     second.start()
+    copy(xs.at[2, 1], xr.at[LEFT, 1, 1], TO_X, FROM_LEFT + 4, to_right).start()
     own(1)
-    copy(xs.at[1], xr.at[LEFT, 2], TO_X, FROM_LEFT + 3, to_right).start()
+    copy(xs.at[1], xr.at[LEFT, 2], TO_X, FROM_LEFT + 5, to_right).start()
     own(0)
-    copy(xs.at[0, :, LEFT_PART], xr.at[LEFT, 3, :, LEFT_PART], TO_X, FROM_LEFT + 3, to_right).start()
+    copy(xs.at[0, :, LEFT_PART], xr.at[LEFT, 3, :, LEFT_PART], TO_X, FROM_LEFT + 5, to_right).start()
     start_y(lambda d, h, sent: [copy(ms.at[:, h], myr.at[d], sent, FROM_Y + d, (gx, row_of(d)))])
     second.wait_send()
     start_y(lambda d, h, sent: [
@@ -258,21 +263,27 @@
     for k in range(1, 5):
         unpack(RIGHT, k)
 
-    loop(3, lambda i: column_steps(grid, masks, 0, (5 + 2 * i, 6 + 2 * i)))
+    def pass_on(k, h):
+        arrive(FROM_LEFT + 2 * k - 1 + h, UNITS["corner"])
+        d = 1 - h
+
+        @pl.when(has[h])
+        def _():
+            copy(xr.at[LEFT, k - 1, h], cr.at[d, LEFT, k - 1], TO_ABOVE if d == BELOW else TO_BELOW, LEFT_CORNER + 4 * d + k,
+                 (gx, row_of(d))).start()
+
+    pass_on(1, 0)
 
     @pl.when(seam)
     def _():
         meet_left()
 
-    def pass_on(k):
-        arrive(FROM_LEFT + k, UNITS["column"])
-        start_y(lambda d, h, sent: [
-            copy(xr.at[LEFT, k - 1, h], cr.at[d, LEFT, k - 1], sent, LEFT_CORNER + 4 * d + k, (gx, row_of(d)))])
-
-    pass_on(1)
+    loop(3, lambda i: column_steps(grid, masks, 0, (5 + 2 * i, 6 + 2 * i)))
+    pass_on(1, 1)
     loop(2, lambda i: column_steps(grid, masks, 1, (6 + 2 * i, 7 + 2 * i)))
-    pass_on(2)
+    pass_on(2, 0)
     column_steps(grid, masks, 2, (7, 8))
+    pass_on(2, 1)
 
     wait_y(LEFT_CORNER, 4, 4)
     unpack_marks(LEFT)
@@ -284,20 +295,25 @@
         for q in range(19):
             out_ref[q, c] = jnp.where(wet, f[q], f0[q, c])
 
-    for k in (1, 2):
-        wait_y(LEFT_CORNER + k, 4, UNITS["corner"])
+    wait_y(LEFT_CORNER + 1, 4, UNITS["corner"])
+    unpack(LEFT, 1)
+    loop(3, lambda level: column_steps(grid, masks, level, (level + 4,)))
+    finish(3)
+    arrive(FROM_LEFT + 5, UNITS["far"])
+    wait_y(LEFT_CORNER + 2, 4, UNITS["corner"])
+    wait_y(LEFT_CORNER + 3, 4, UNITS["far_corner"])
+    for k in (2, 3, 4):
         unpack(LEFT, k)
-        loop(3, lambda level: column_steps(grid, masks, level, (level + 5 - k,)))
-        finish(4 - k)
-    arrive(FROM_LEFT + 3, UNITS["far"])
-    wait_y(LEFT_CORNER + 3, 4, UNITS["far_corner"])
-    unpack(LEFT, 3)
-    unpack(LEFT, 4)
-    loop(3, lambda level: column_steps(grid, masks, level, (level + 1, level + 2)))
-    finish(1)
-    finish(0)
-
-    departed(TO_X, 8 + 38 + UNITS["far"] + 8 + UNITS["all"])
+
+    def last_wave(level):
+        column_steps(grid, masks, level, (level + 1,), ORDER[14:])
+        column_steps(grid, masks, level, (level + 2, level + 3))
+
+    loop(3, last_wave)
+    for c in (2, 1, 0):
+        finish(c)
+
+    departed(TO_X, 8 + 38 + 19 + UNITS["far"] + 8 + UNITS["all"])
     for d in (BELOW, ABOVE):
         @pl.when(has[1 - d])
         def _():

time: 29.3 us -> 29 us (0.990)
  Pallas kernels: 28.4 us -> 28 us
    pallas_call x1, Pallas kernels: 28.4 us -> 28 us  [per_device(): pl.pallas_call(functools.partial(kernel, nx, ny, zs), out_shape=pltpu.VME...]
where the time goes in v3:
time: 29 us; the launch traced here: 28.8 us
  Pallas kernels  28 us (97%)
  local copies, waits for them, and re-layouts  0.72 us (2%)
    pallas_call x1, Pallas kernels, per_device(): pl.pallas_call(functools.partial(kernel, nx, ny, zs), out_shape=pltpu.VME...  28 us
    unnamed x1, local copies, waits for them, and re-layouts  0.72 us

profile of v3, /device:TPU:2, one launch (start us, length us, event | category | flops | bytes accessed | tf_op | source)
XLA Modules:
  0.0 28.8 jit_solution(7673242936714523781)
XLA Ops:
  0.0 28.0 %shard_map.28 = f32[19,4,8,128]{3,2,1,0:T(8,128)S(1)} custom-call(f32[19,4,8,128]{3,2,1,0:T(8,128)} %pop_ref.1, s32[4,8,128]{2,1,0:T(8,128)} %fluid_ref.1), custom_call_target="tpu_custom_call" | custom-call | tf_op jit(solution)/shard_map/pallas_call | solution.py:328
  28.0 0.7 %copy.4 = f32[19,4,8,128]{3,2,1,0:T(8,128)} copy(f32[19,4,8,128]{3,2,1,0:T(8,128)S(1)} %shard_map.28) | data formatting | bytes 622592

commit v4 on v3

--- a/solution.py
+++ b/solution.py
@@ -99,17 +99,20 @@
 FROM_Y = 8
 LEFT_CORNER = 10
 RIGHT_CORNER = 18
-ARRIVALS = 22
-TO_X, TO_X_SECOND, TO_ABOVE, TO_BELOW = range(4)
+RELAY = 22
+ARRIVALS = 26
+TO_X, TO_X_SECOND, TO_ABOVE, TO_BELOW, NEAR_ABOVE, NEAR_BELOW, RELAYED = range(7)
 UNITS = {"column": 38, "far": 48, "all": 124, "rows": 80, "corner": 19, "far_corner": 24, "all_corner": 62}
 
 
-def kernel(nx, ny, zs, pop_ref, fluid_ref, out_ref, f0, wet_in, xs, ms, xr, mxr, yr, myr, cr, mcr, grid, marks, masks, units,
+def kernel(nx, ny, zs, pop_ref, fluid_ref, out_ref, f0, wet_in, xs, ms, xr, mxr, yr, myr, cr, mcr, grid, marks, masks, units, relay,
            load_sem, send_sem, recv_sem):
     gx, gy = lax.axis_index("gx"), lax.axis_index("gy")
     right, left = lax.rem(gx + 1, nx), lax.rem(gx + nx - 1, nx)
     has = (gy > 0, gy < ny - 1)
-    seam = lax.rem(gx, zs) == 0
+    place = lax.rem(gx, zs)
+    seam, helper, late = place == 0, place == 1, place == zs - 1
+    right2, left2 = lax.rem(gx + 2, nx), lax.rem(gx + nx - 2, nx)
 
     barrier = pltpu.get_barrier_semaphore()
     for d, step in ((BELOW, -1), (ABOVE, 1)):
@@ -118,6 +121,10 @@
             pl.semaphore_signal(barrier, inc=1, device_id=(gx, gy + step), device_id_type=MESH)
             pl.semaphore_signal(barrier, inc=1, device_id=(left, gy + step), device_id_type=MESH)
     pl.semaphore_signal(barrier, inc=1, device_id=(left, gy), device_id_type=MESH)
+
+    @pl.when(helper)
+    def _():
+        pl.semaphore_signal(barrier, inc=1, device_id=(left2, gy), device_id_type=MESH)
 
     load_fluid = pltpu.make_async_copy(fluid_ref, wet_in, load_sem.at[0])
     load_last = pltpu.make_async_copy(pop_ref.at[:, pl.ds(3, 1)], f0.at[:, pl.ds(3, 1)], load_sem.at[1])
@@ -179,27 +186,43 @@
 
     load_last.wait()
     own(3)
-    pl.semaphore_wait(barrier, 1 + 2 * ((gy + ny - 1) // ny) + 2 * ((2 * ny - 2 - gy) // ny))
+    beside = (gy + ny - 1) // ny + (2 * ny - 2 - gy) // ny
+    pl.semaphore_wait(barrier, 1 + 2 * beside + place // (zs - 1))
     to_right = (right, gy)
-    copy(xs.at[3, 0], xr.at[LEFT, 0, 0], TO_X, FROM_LEFT + 1, to_right).start()
+
+    def near(k, h, sent):
+        @pl.when(late)
+        def _():
+            copy(xs.at[4 - k, h], relay.at[k - 1, h], sent, RELAY + 2 * k - 2 + h, (right2, gy)).start()
+
+        @pl.when(jnp.logical_not(late))
+        def _():
+            copy(xs.at[4 - k, h], xr.at[LEFT, k - 1, h], sent, FROM_LEFT + 2 * k - 1 + h, to_right).start()
+
+    near(1, 0, TO_X_SECOND)
     copy(ms, mxr.at[LEFT], TO_X, FROM_LEFT, to_right).start()
-    copy(xs.at[3, 1], xr.at[LEFT, 0, 1], TO_X, FROM_LEFT + 2, to_right).start()
+    near(1, 1, TO_X)
     load_rest.wait()
     own(2)
-    second = copy(xs.at[2, 0], xr.at[LEFT, 1, 0], TO_X_SECOND, FROM_LEFT + 3, to_right)
-    second.start()
-    copy(xs.at[2, 1], xr.at[LEFT, 1, 1], TO_X, FROM_LEFT + 4, to_right).start()
+    near(2, 0, TO_X)
+    near(2, 1, TO_X)
     own(1)
     copy(xs.at[1], xr.at[LEFT, 2], TO_X, FROM_LEFT + 5, to_right).start()
     own(0)
     copy(xs.at[0, :, LEFT_PART], xr.at[LEFT, 3, :, LEFT_PART], TO_X, FROM_LEFT + 5, to_right).start()
     start_y(lambda d, h, sent: [copy(ms.at[:, h], myr.at[d], sent, FROM_Y + d, (gx, row_of(d)))])
-    second.wait_send()
+    departed(TO_X_SECOND, UNITS["corner"])
     start_y(lambda d, h, sent: [
         copy(xs.at[1, h], cr.at[d, LEFT, 2], sent, LEFT_CORNER + 4 * d + 3, (right, row_of(d))),
         copy(xs.at[0, h, LEFT_PART], cr.at[d, LEFT, 3, LEFT_PART], sent, LEFT_CORNER + 4 * d + 3, (right, row_of(d))),
-        copy(xs.at[:, h], yr.at[d], sent, FROM_Y + d, (gx, row_of(d))),
     ])
+
+    def send_rows():
+        start_y(lambda d, h, sent: [copy(xs.at[:, h], yr.at[d], sent, FROM_Y + d, (gx, row_of(d)))])
+
+    @pl.when(place < zs - 2)
+    def _():
+        send_rows()
 
     def meet_left():
         arrive(FROM_LEFT, 8)
@@ -213,6 +236,10 @@
     @pl.when(jnp.logical_not(seam))
     def _():
         meet_left()
+
+    @pl.when(place >= zs - 2)
+    def _():
+        send_rows()
 
     def unpack_marks(side):
         for c in range(4):
@@ -264,12 +291,15 @@
         unpack(RIGHT, k)
 
     def pass_on(k, h):
-        arrive(FROM_LEFT + 2 * k - 1 + h, UNITS["corner"])
         d = 1 - h
 
-        @pl.when(has[h])
-        def _():
-            copy(xr.at[LEFT, k - 1, h], cr.at[d, LEFT, k - 1], TO_ABOVE if d == BELOW else TO_BELOW, LEFT_CORNER + 4 * d + k,
+        @pl.when(jnp.logical_not(seam))
+        def _():
+            arrive(FROM_LEFT + 2 * k - 1 + h, UNITS["corner"])
+
+        @pl.when(jnp.logical_and(jnp.logical_not(seam), has[h]))
+        def _():
+            copy(xr.at[LEFT, k - 1, h], cr.at[d, LEFT, k - 1], NEAR_ABOVE if d == BELOW else NEAR_BELOW, LEFT_CORNER + 4 * d + k,
                  (gx, row_of(d))).start()
 
     pass_on(1, 0)
@@ -285,6 +315,25 @@
     column_steps(grid, masks, 2, (7, 8))
     pass_on(2, 1)
 
+    @pl.when(helper)
+    def _():
+        for k in (1, 2):
+            for h in (0, 1):
+                arrive(RELAY + 2 * k - 2 + h, UNITS["corner"])
+                d = 1 - h
+
+                @pl.when(has[h])
+                def _():
+                    copy(relay.at[k - 1, h], cr.at[d, LEFT, k - 1], RELAYED, LEFT_CORNER + 4 * d + k, (left, row_of(d))).start()
+
+                copy(relay.at[k - 1, h], xr.at[LEFT, k - 1, h], RELAYED, FROM_LEFT + 2 * k - 1 + h, (left, gy)).start()
+
+    def near_arrived(k):
+        @pl.when(seam)
+        def _():
+            for h in (0, 1):
+                arrive(FROM_LEFT + 2 * k - 1 + h, UNITS["corner"])
+
     wait_y(LEFT_CORNER, 4, 4)
     unpack_marks(LEFT)
     loop(2, lambda i: mask_columns(marks, masks, (1 + 2 * i, 2 + 2 * i)))
@@ -295,15 +344,18 @@
         for q in range(19):
             out_ref[q, c] = jnp.where(wet, f[q], f0[q, c])
 
+    near_arrived(1)
     wait_y(LEFT_CORNER + 1, 4, UNITS["corner"])
     unpack(LEFT, 1)
     loop(3, lambda level: column_steps(grid, masks, level, (level + 4,)))
     finish(3)
+    near_arrived(2)
+    wait_y(LEFT_CORNER + 2, 4, UNITS["corner"])
+    unpack(LEFT, 2)
     arrive(FROM_LEFT + 5, UNITS["far"])
-    wait_y(LEFT_CORNER + 2, 4, UNITS["corner"])
     wait_y(LEFT_CORNER + 3, 4, UNITS["far_corner"])
-    for k in (2, 3, 4):
-        unpack(LEFT, k)
+    unpack(LEFT, 3)
+    unpack(LEFT, 4)
 
     def last_wave(level):
         column_steps(grid, masks, level, (level + 1,), ORDER[14:])
@@ -319,7 +371,21 @@
         def _():
             departed(
                 TO_ABOVE if d == BELOW else TO_BELOW,
-                UNITS["rows"] + 4 + 2 * UNITS["corner"] + UNITS["far_corner"] + 4 + UNITS["all_corner"])
+                UNITS["rows"] + 4 + UNITS["far_corner"] + 4 + UNITS["all_corner"])
+
+        @pl.when(jnp.logical_and(jnp.logical_not(seam), has[1 - d]))
+        def _():
+            departed(NEAR_ABOVE if d == BELOW else NEAR_BELOW, 2 * UNITS["corner"])
+
+    both = jnp.logical_and(has[BELOW], has[ABOVE])
+
+    @pl.when(jnp.logical_and(helper, both))
+    def _():
+        departed(RELAYED, 8 * UNITS["corner"])
+
+    @pl.when(jnp.logical_and(helper, jnp.logical_not(both)))
+    def _():
+        departed(RELAYED, 6 * UNITS["corner"])
 
 
 def per_device(nx, ny, zs, populations, fluid):
@@ -345,8 +411,9 @@
             vm(12, 16, 128),
             vm(12, 18, 16, 128),
             vm(256, 4, 128),
+            vm(2, 2, 19, 4, 128),
             pltpu.SemaphoreType.DMA((3,)),
-            pltpu.SemaphoreType.DMA((4,)),
+            pltpu.SemaphoreType.DMA((7,)),
             pltpu.SemaphoreType.DMA((ARRIVALS,)),
         ],
         compiler_params=pltpu.CompilerParams(

time: 29 us -> 28.6 us (0.986)
  Pallas kernels: 28 us -> 27.6 us
    pallas_call x1, Pallas kernels: 28 us -> 27.6 us  [per_device(): pl.pallas_call(functools.partial(kernel, nx, ny, zs), out_shape=pltpu.VME...]
where the time goes in v4:
time: 28.6 us; the launch traced here: 28.4 us
  Pallas kernels  27.6 us (97%)
  local copies, waits for them, and re-layouts  0.72 us (3%)
    pallas_call x1, Pallas kernels, per_device(): pl.pallas_call(functools.partial(kernel, nx, ny, zs), out_shape=pltpu.VME...  27.6 us
    unnamed x1, local copies, waits for them, and re-layouts  0.72 us

profile of v4, /device:TPU:2, one launch (start us, length us, event | category | flops | bytes accessed | tf_op | source)
XLA Modules:
  0.0 28.4 jit_solution(8312108075525167142)
XLA Ops:
  0.0 27.6 %shard_map.28 = f32[19,4,8,128]{3,2,1,0:T(8,128)S(1)} custom-call(f32[19,4,8,128]{3,2,1,0:T(8,128)} %pop_ref.1, s32[4,8,128]{2,1,0:T(8,128)} %fluid_ref.1), custom_call_target="tpu_custom_call" | custom-call | tf_op jit(solution)/shard_map/pallas_call | solution.py:394
  27.7 0.7 %copy.4 = f32[19,4,8,128]{3,2,1,0:T(8,128)} copy(f32[19,4,8,128]{3,2,1,0:T(8,128)S(1)} %shard_map.28) | data formatting | bytes 622592

commit v5 on v4

--- a/solution.py
+++ b/solution.py
@@ -249,12 +249,19 @@
             marks[col, pl.ds(0, 4), :] = mcr[BELOW, side, c]
             marks[col, pl.ds(12, 4), :] = mcr[ABOVE, side, c]
 
-    def unpack(side, k):
-        c = 4 - k if side == LEFT else 8 + k - 1
+    def place_of(side, k):
         slots = range(19) if k < 4 else (range(14, 19) if side == LEFT else range(5))
+        return 4 - k if side == LEFT else 8 + k - 1, slots
+
+    def unpack_own_rows(side, k):
+        c, slots = place_of(side, k)
         for s in slots:
             grid[0, c, s, pl.ds(4, 4), :] = xr[side, k - 1, 0, s]
             grid[0, c, s, pl.ds(8, 4), :] = xr[side, k - 1, 1, s]
+
+    def unpack_corners(side, k):
+        c, slots = place_of(side, k)
+        for s in slots:
             grid[0, c, s, pl.ds(0, 4), :] = cr[BELOW, side, k - 1, s]
             grid[0, c, s, pl.ds(12, 4), :] = cr[ABOVE, side, k - 1, s]
 
@@ -288,7 +295,8 @@
     loop(3, lambda i: mask_columns(marks, masks, (5 + 2 * i, 6 + 2 * i)))
     wait_y(RIGHT_CORNER + 1, 2, UNITS["all_corner"])
     for k in range(1, 5):
-        unpack(RIGHT, k)
+        unpack_own_rows(RIGHT, k)
+        unpack_corners(RIGHT, k)
 
     def pass_on(k, h):
         d = 1 - h
@@ -345,17 +353,19 @@
             out_ref[q, c] = jnp.where(wet, f[q], f0[q, c])
 
     near_arrived(1)
+    near_arrived(2)
+    arrive(FROM_LEFT + 5, UNITS["far"])
+    for k in range(1, 5):
+        unpack_own_rows(LEFT, k)
     wait_y(LEFT_CORNER + 1, 4, UNITS["corner"])
-    unpack(LEFT, 1)
+    unpack_corners(LEFT, 1)
     loop(3, lambda level: column_steps(grid, masks, level, (level + 4,)))
     finish(3)
-    near_arrived(2)
     wait_y(LEFT_CORNER + 2, 4, UNITS["corner"])
-    unpack(LEFT, 2)
-    arrive(FROM_LEFT + 5, UNITS["far"])
+    unpack_corners(LEFT, 2)
     wait_y(LEFT_CORNER + 3, 4, UNITS["far_corner"])
-    unpack(LEFT, 3)
-    unpack(LEFT, 4)
+    unpack_corners(LEFT, 3)
+    unpack_corners(LEFT, 4)
 
     def last_wave(level):
         column_steps(grid, masks, level, (level + 1,), ORDER[14:])

time: 28.6 us -> 28.6 us (level)
  no operation moved by 1% of the time
where the time goes in v5:
time: 28.6 us; the launch traced here: 28.4 us
  Pallas kernels  27.6 us (97%)
  local copies, waits for them, and re-layouts  0.72 us (3%)
    pallas_call x1, Pallas kernels, per_device(): pl.pallas_call(functools.partial(kernel, nx, ny, zs), out_shape=pltpu.VME...  27.6 us
    unnamed x1, local copies, waits for them, and re-layouts  0.72 us

profile of v5, /device:TPU:2, one launch (start us, length us, event | category | flops | bytes accessed | tf_op | source)
XLA Modules:
  0.0 28.4 jit_solution(8504973846317091832)
XLA Ops:
  0.0 27.6 %shard_map.28 = f32[19,4,8,128]{3,2,1,0:T(8,128)S(1)} custom-call(f32[19,4,8,128]{3,2,1,0:T(8,128)} %pop_ref.1, s32[4,8,128]{2,1,0:T(8,128)} %fluid_ref.1), custom_call_target="tpu_custom_call" | custom-call | tf_op jit(solution)/shard_map/pallas_call | solution.py:404
  27.6 0.7 %copy.4 = f32[19,4,8,128]{3,2,1,0:T(8,128)} copy(f32[19,4,8,128]{3,2,1,0:T(8,128)S(1)} %shard_map.28) | data formatting | bytes 622592
